TPU v7x, 32 devices: a whole 2x2x4 slice. The times are simulated.
32 devices in a mesh: col: 8 (over y, x, core), row: 4 (over z).
Axes of the slice: x: 2, y: 2, z: 4, core: 2. Of those that a mesh axis runs over, the one named last changes fastest.
Arguments:
- visibilities: bfloat16 [2, 8192, 4096], P(None, 'col', 'row'), may hold values from -6 to 6
- col_offsets: int32 [8], P('col'), may hold values from 0 to 15360
- row_offsets: int32 [4], replicated, may hold values from 0 to 15360
- facet_offsets: int32 [8, 2], replicated, may hold values from 0 to 16383
- facet_order: int32 [8], replicated, may hold values from 0 to 7, each once
- vis_counts: int32 [8, 4], P('col', 'row'), may hold values from 512 to 1024
Outputs:
- facet_images: float32 [8, 2, 64, 4096], P('col', None, None, 'row')
- peak: float32 [8], P('col')
Inputs may be any that keep to these rules, and one draw needn't show every extreme that they name: `facet_order`: each slot names a different facet.
All inputs are finite; a program needn't handle non-finite values.
Results may differ from a plain program's by a relative error of at most 0.0078.
Values may be sent and summed in bfloat16 or wider, within the bound.
A program may use at most 128 MiB of HBM per device.

v0:
```python
import functools
import math

import jax
import jax.numpy as jnp
from jax import lax
from jax.experimental import pallas as pl
from jax.experimental.pallas import tpu as pltpu
from jax.sharding import PartitionSpec as P

FS = 4096
NG = 16384
FR = 64
TWO_PI = 2.0 * math.pi
BEAM_SLOPE = 0.66
FINE = 32
CHUNKS = 4
MESH = pl.DeviceIdType.MESH
F32 = jnp.float32
BF16 = jnp.bfloat16


def cis(product):
    shift = (NG // 4).bit_length() - 1
    turn = product & (NG - 1)
    quadrant = (turn + NG // 8) >> shift
    rest = turn - (quadrant << shift)
    angle = rest.astype(F32) * (TWO_PI / NG)
    z = angle * angle
    sine = angle * (1.0 + z * (-1.0 / 6 + z * (1.0 / 120 + z * (-1.0 / 5040 + z * (1.0 / 362880)))))
    cosine = 1.0 + z * (-0.5 + z * (1.0 / 24 + z * (-1.0 / 720 + z * (1.0 / 40320))))
    odd = (quadrant & 1) == 1
    real = jnp.where(odd, sine, cosine)
    imag = jnp.where(odd, cosine, sine)
    real = jnp.where(((quadrant + 1) & 2) != 0, -real, real)
    imag = jnp.where((quadrant & 2) != 0, -imag, imag)
    return real, imag


def iota(shape, dim):
    return lax.broadcasted_iota(jnp.int32, shape, dim)


def kernel(
    cols, rows,
    vis_hbm, *refs,
):
    small, (image, peak), scratch = refs[:5], refs[5:7], refs[7:]
    (
    col_off, row_off, facet_off, facet_order, counts, small_sem,
    vis, head, fine, table, mine, pair_out, pair_in, sums, others, gathered,
    coarse2, fine2, table2, totals, peaks,
    vis_sem, pair_send, pair_recv, col_send, col_recv, row_send, row_recv, peak_send, peak_recv,
    ) = scratch
    copies = [
        pltpu.make_async_copy(source, target, small_sem.at[n])
        for n, (source, target) in enumerate(zip(small, scratch[:5]))
    ]
    for copy in copies:
        copy.start()
    m = vis.shape[1]
    width = m // CHUNKS
    chips = cols // 2
    block_cols = FS // rows
    me_col = lax.axis_index("col")
    me_row = lax.axis_index("row")
    core = lax.rem(me_col, 2)
    chip = me_col // 2
    partner = chip * 2 + 1 - core

    def peer_chip(d):
        return lax.rem(chip + d, chips) * 2 + core

    def peer_row(d):
        return lax.rem(me_row + d, rows)

    barrier = pltpu.get_barrier_semaphore()
    pl.semaphore_signal(barrier, inc=1, device_id=(partner, me_row), device_id_type=MESH)
    for d in range(1, chips):
        pl.semaphore_signal(barrier, inc=1, device_id=(peer_chip(d), me_row), device_id_type=MESH)
    for d in range(1, rows):
        pl.semaphore_signal(barrier, inc=1, device_id=(me_col, peer_row(d)), device_id_type=MESH)

    def vis_copy(k):
        part = pl.ds(k * width, width)
        return pltpu.make_async_copy(vis_hbm.at[:, :, part], vis.at[:, :, part], vis_sem.at[k])

    for k in range(CHUNKS):
        vis_copy(k).start()

    for copy in copies:
        copy.wait()

    u = iota((cols, m), 1)
    slot = iota((cols, m), 0)
    start = jnp.zeros((cols, m), jnp.int32)
    for half in range(2):
        for c in range(chips):
            facet = facet_order[c * 2 + (core if half == 0 else 1 - core)]
            first = (facet_off[0, facet] + (FS // 2 - FR // 2)) & (NG - 1)
            start = jnp.where(slot == half * chips + c, first, start)
    real, imag = cis(start * (col_off[0] + u))
    scale = jnp.where(u < counts[0, 0], 1.0 / math.sqrt(m * cols), 0.0)
    head[0] = real * scale
    head[1] = imag * scale
    real, imag = cis(iota((FR, m), 0) * (col_off[0] + iota((FR, m), 1)))
    fine[0] = real
    fine[1] = imag
    def column_table(half):
        block = chips * FR
        for at in range(chips):
            s = half * chips + at
            a, b = head[0, pl.ds(s, 1), :], head[1, pl.ds(s, 1), :]
            c, d = fine[0], fine[1]
            imag = a * d + b * c
            table[half, pl.ds(at * FR, FR), :] = (-imag).astype(BF16)
            table[half, pl.ds(block + at * FR, FR), :] = (a * c - b * d).astype(BF16)
            table[half, pl.ds(2 * block + at * FR, FR), :] = imag.astype(BF16)

    def pair_copy(k):
        return pltpu.make_async_remote_copy(
            src_ref=pair_out.at[k], dst_ref=pair_in.at[k],
            send_sem=pair_send.at[k], recv_sem=pair_recv.at[k],
            device_id=(partner, me_row), device_id_type=MESH)

    def col_copy(k, d):
        target = lax.rem(chip + d, chips)
        return pltpu.make_async_remote_copy(
            src_ref=sums.at[k, target], dst_ref=others.at[k, d - 1],
            send_sem=col_send.at[k, d - 1], recv_sem=col_recv.at[k, d - 1],
            device_id=(target * 2 + core, me_row), device_id_type=MESH)

    def row_copy(k, origin, step):
        side = 0 if step > 0 else 1
        return pltpu.make_async_remote_copy(
            src_ref=gathered.at[k, origin], dst_ref=gathered.at[k, origin],
            send_sem=row_send.at[k, side, origin], recv_sem=row_recv.at[k, origin],
            device_id=(me_col, me_row + step), device_id_type=MESH)

    def transform(k, half):
        if half == 1:
            vis_copy(k).wait()
        part = pl.ds(k * width, width)
        block = chips * FR
        dot = functools.partial(jnp.dot, preferred_element_type=F32)
        both = dot(table[half, pl.ds(block, 2 * block), :], vis[0, :, part])
        both += dot(table[half, pl.ds(0, 2 * block), :], vis[1, :, part])
        pr = both[:block].reshape(chips, FR, width)
        pi = both[block:].reshape(chips, FR, width)
        if half == 1:
            pair_out[k, :, pl.ds(0, FR), :] = pr.astype(BF16)
            pair_out[k, :, pl.ds(FR, FR), :] = pi.astype(BF16)
            if k == 0:
                pl.semaphore_wait(barrier, chips + rows - 1)
            pair_copy(k).start()
        else:
            mine[k, :, pl.ds(0, FR), :] = pr
            mine[k, :, pl.ds(FR, FR), :] = pi

    def pair_sum(k):
        pair_copy(k).wait_recv()
        sums[k] = (mine[k] + pair_in[k].astype(F32)).astype(BF16)
        for d in range(1, chips):
            col_copy(k, d).start()

    def facet_sum(k):
        total = mine[k, chip] + pair_in[k, chip].astype(F32)
        for d in range(1, chips):
            col_copy(k, d).wait_recv()
            total = total + others[k, d - 1].astype(F32)
        gathered[k, me_row] = total.astype(BF16)

        @pl.when(me_row < rows - 1)
        def _():
            row_copy(k, me_row, 1).start()

        @pl.when(me_row > 0)
        def _():
            row_copy(k, me_row, -1).start()

    def relay(k, dist):
        @pl.when(me_row - dist >= 0)
        def _():
            row_copy(k, me_row - dist, 1).wait_recv()

            @pl.when(me_row < rows - 1)
            def _():
                row_copy(k, me_row - dist, 1).start()

        @pl.when(me_row + dist < rows)
        def _():
            row_copy(k, me_row + dist, -1).wait_recv()

            @pl.when(me_row > 0)
            def _():
                row_copy(k, me_row + dist, -1).start()

    def second(k):
        left = gathered[k].reshape(rows * 2 * FR, width)
        part = pl.ds(k * width, width)
        for side in range(2):
            product = jnp.dot(left, table2[side, part, :], preferred_element_type=F32)
            if k == 0:
                totals[side] = product
            else:
                totals[side] += product

    column_table(1)
    transform(0, 1)
    column_table(0)
    transform(0, 0)
    for k in range(1, CHUNKS):
        transform(k, 1)
        pair_sum(k - 1)
        transform(k, 0)
    pair_sum(CHUNKS - 1)
    facet_sum(0)

    own_facet = facet_order[me_col]
    column0 = (facet_off[1, own_facet] + me_row * block_cols) & (NG - 1)
    shape = (m // FINE, block_cols)
    real, imag = cis(iota(shape, 0) * FINE * (column0 + iota(shape, 1)))
    coarse2[0] = real
    coarse2[1] = imag
    shape = (FINE, block_cols)
    real, imag = cis(iota(shape, 0) * (column0 + iota(shape, 1)))
    fine2[0] = real
    fine2[1] = imag

    def row_table(h, carry):
        a, b = coarse2[0, pl.ds(h, 1), :], coarse2[1, pl.ds(h, 1), :]
        c, d = fine2[0], fine2[1]
        out = pl.ds(pl.multiple_of(h * FINE, FINE), FINE)
        table2[0, out, :] = (a * c - b * d).astype(BF16)
        table2[1, out, :] = (a * d + b * c).astype(BF16)
        return carry

    lax.fori_loop(0, m // FINE, row_table, 0)

    row_ids = iota((rows, block_cols), 0)
    offsets = jnp.zeros((rows, block_cols), jnp.int32)
    for r in range(rows):
        offsets = jnp.where(row_ids == r, row_off[r], offsets)
    lanes = iota((rows, block_cols), 1)
    beam = 1.0 - BEAM_SLOPE * ((me_row * block_cols + lanes).astype(F32) + 0.5) / FS
    gain = (0.5 / math.sqrt(m * rows)) / beam
    phase_real, phase_imag = cis(offsets * ((column0 + lanes) & (NG - 1)))
    phase_real, phase_imag = phase_real * gain, phase_imag * gain

    for step in range(CHUNKS + rows - 1):
        if 0 < step < CHUNKS:
            facet_sum(step)
        for dist in range(1, rows):
            k = step - dist
            if 0 <= k < CHUNKS:
                relay(k, dist)
                if dist == rows - 1:
                    second(k)

    out_real = jnp.zeros((FR, block_cols), F32)
    out_imag = jnp.zeros((FR, block_cols), F32)
    for r in range(rows):
        top, low = pl.ds(r * 2 * FR, FR), pl.ds(r * 2 * FR + FR, FR)
        real = totals[0, top, :] - totals[1, low, :]
        imag = totals[1, top, :] + totals[0, low, :]
        a, b = phase_real[r : r + 1], phase_imag[r : r + 1]
        out_real = out_real + (real * a - imag * b)
        out_imag = out_imag + (real * b + imag * a)
    image[0, 0] = out_real
    image[0, 1] = out_imag
    power = out_real * out_real + out_imag * out_imag
    power = jnp.max(power.reshape(FR // 8, 8, block_cols), axis=0)
    best = power[:, :128]
    for n in range(1, block_cols // 128):
        best = jnp.maximum(best, power[:, n * 128 : (n + 1) * 128])
    peaks[me_row] = jnp.sqrt(best)

    def peak_copy(d):
        return pltpu.make_async_remote_copy(
            src_ref=peaks.at[me_row], dst_ref=peaks.at[me_row],
            send_sem=peak_send.at[d - 1], recv_sem=peak_recv.at[d - 1],
            device_id=(me_col, peer_row(d)), device_id_type=MESH)

    for d in range(1, rows):
        peak_copy(d).start()

    for k in range(CHUNKS):
        pair_copy(k).wait_send()
        for d in range(1, chips):
            col_copy(k, d).wait_send()

        @pl.when(me_row < rows - 1)
        def _():
            row_copy(k, me_row, 1).wait_send()

        @pl.when(me_row > 0)
        def _():
            row_copy(k, me_row, -1).wait_send()

        for dist in range(1, rows):
            @pl.when((me_row - dist >= 0) & (me_row < rows - 1))
            def _():
                row_copy(k, me_row - dist, 1).wait_send()

            @pl.when((me_row + dist < rows) & (me_row > 0))
            def _():
                row_copy(k, me_row + dist, -1).wait_send()

    for d in range(1, rows):
        peak_copy(d).wait()
    best = peaks[0]
    for r in range(1, rows):
        best = jnp.maximum(best, peaks[r])
    peak[0] = jnp.max(best)


def local(cols, rows, visibilities, col_offsets, row_offsets, facet_offsets, facet_order, vis_counts):
    m = visibilities.shape[1]
    width = m // CHUNKS
    chips = cols // 2
    block_cols = FS // rows
    dma = pltpu.SemaphoreType.DMA
    smem = pl.BlockSpec(memory_space=pltpu.SMEM)
    anywhere = pl.BlockSpec(memory_space=pl.ANY)
    small = (col_offsets, row_offsets, facet_offsets.T, facet_order, vis_counts)
    return pl.pallas_call(
        functools.partial(kernel, cols, rows),
        out_shape=(
            pltpu.VMEM((1, 2, FR, block_cols), F32),
            jax.ShapeDtypeStruct((1,), F32),
        ),
        in_specs=[anywhere] * 6,
        out_specs=(pl.BlockSpec(memory_space=pltpu.VMEM), smem),
        scratch_shapes=[pltpu.SMEM(x.shape, x.dtype) for x in small] + [
            dma((len(small),)),
            pltpu.VMEM((2, m, m), BF16),
            pltpu.VMEM((2, cols, m), F32),
            pltpu.VMEM((2, FR, m), F32),
            pltpu.VMEM((2, 3 * chips * FR, m), BF16),
            pltpu.VMEM((CHUNKS, chips, 2 * FR, width), F32),
            pltpu.VMEM((CHUNKS, chips, 2 * FR, width), BF16),
            pltpu.VMEM((CHUNKS, chips, 2 * FR, width), BF16),
            pltpu.VMEM((CHUNKS, chips, 2 * FR, width), BF16),
            pltpu.VMEM((CHUNKS, chips - 1, 2 * FR, width), BF16),
            pltpu.VMEM((CHUNKS, rows, 2 * FR, width), BF16),
            pltpu.VMEM((2, m // FINE, block_cols), F32),
            pltpu.VMEM((2, FINE, block_cols), F32),
            pltpu.VMEM((2, m, block_cols), BF16),
            pltpu.VMEM((2, rows * 2 * FR, block_cols), F32),
            pltpu.VMEM((rows, 8, 128), F32),
            dma((CHUNKS,)),
            dma((CHUNKS,)),
            dma((CHUNKS,)),
            dma((CHUNKS, chips - 1)),
            dma((CHUNKS, chips - 1)),
            dma((CHUNKS, 2, rows)),
            dma((CHUNKS, rows)),
            dma((rows - 1,)),
            dma((rows - 1,)),
        ],
        compiler_params=pltpu.CompilerParams(
            collective_id=0, has_side_effects=True, vmem_limit_bytes=60 * 1024 * 1024),
    )(visibilities, *small)


def solution(mesh):
    in_specs = (P(None, "col", "row"), P("col"), P(), P(), P(), P("col", "row"))
    out_specs = (P("col", None, None, "row"), P("col"))
    body = functools.partial(local, mesh.shape["col"], mesh.shape["row"])
    return jax.shard_map(body, mesh=mesh, in_specs=in_specs, out_specs=out_specs, check_vma=False)
```

profile of v0, /device:TPU:0, one launch (start us, length us, event | category | flops | bytes accessed | tf_op | source)
XLA Modules:
  0.0 44.3 jit_solution(5105515084579326576)
XLA Ops:
  1.9 39.8 %shard_map.77 = (f32[1,2,64,1024]{3,2,1,0:T(8,128)S(1)}, f32[1]{0:T(128)}) custom-call(bf16[2,1024,1024]{2,1,0:T(8,128)(2,1)} %vis_hbm.1, s32[1]{0:T(128)S(6)} %copy.11.refs_0_, s32[4]{0:T(128)} %refs_1_.1, s32[2,8]{1,0:T(2,128)} %bitcast.1, s32[8]{0:T(128)} %refs_3_.1, s32[1,1]{1,0:T(1,128)S(6)} %copy.12.refs_4_), custom_call_target="tpu_custom_call" | custom-call | tf_op jit(solution)/shard_map/pallas_call | solution.py:326
  41.8 0.8 %copy.10 = f32[1,2,64,1024]{3,2,1,0:T(8,128)} copy(f32[1,2,64,1024]{3,2,1,0:T(8,128)S(1)} %get-tuple-element.2) | data formatting | bytes 1048576
where the time goes:
time: 44.4 us; the launch traced here: 44.3 us
  Pallas kernels  39.8 us (90%)
  between operations  3.62 us (8%)
  local copies, waits for them, and re-layouts  0.8 us (2%)
    pallas_call x1, Pallas kernels, local(): pl.pallas_call(functools.partial(kernel, cols, rows), out_shape=(pltpu.VM...  39.8 us

commit v1 on v0

v1 whole, which is shorter than its diff:
```python
import functools
import math

import jax
import jax.numpy as jnp
from jax import lax
from jax.experimental import pallas as pl
from jax.experimental.pallas import tpu as pltpu
from jax.sharding import PartitionSpec as P

FS = 4096
NG = 16384
FR = 64
TWO_PI = 2.0 * math.pi
BEAM_SLOPE = 0.66
FINE = 32
GROUPS = 4
HALVES = 2
CHUNKS = GROUPS * HALVES
MESH = pl.DeviceIdType.MESH
F32 = jnp.float32
BF16 = jnp.bfloat16


def cis(product):
    shift = (NG // 4).bit_length() - 1
    turn = product & (NG - 1)
    quadrant = (turn + NG // 8) >> shift
    rest = turn - (quadrant << shift)
    angle = rest.astype(F32) * (TWO_PI / NG)
    z = angle * angle
    sine = angle * (1.0 + z * (-1.0 / 6 + z * (1.0 / 120 + z * (-1.0 / 5040 + z * (1.0 / 362880)))))
    cosine = 1.0 + z * (-0.5 + z * (1.0 / 24 + z * (-1.0 / 720 + z * (1.0 / 40320))))
    odd = (quadrant & 1) == 1
    real = jnp.where(odd, sine, cosine)
    imag = jnp.where(odd, cosine, sine)
    real = jnp.where(((quadrant + 1) & 2) != 0, -real, real)
    imag = jnp.where((quadrant & 2) != 0, -imag, imag)
    return real, imag


def iota(shape, dim):
    return lax.broadcasted_iota(jnp.int32, shape, dim)


def kernel(
    cols, rows,
    vis_hbm, *refs,
):
    small, (image, peak), scratch = refs[:5], refs[5:7], refs[7:]
    (
    col_off, row_off, facet_off, facet_order, counts, small_sem,
    vis, head, fine, table, mine, pair_out, pair_in, sums, others, gathered,
    coarse2, fine2, table2, phases, relay_out, relay_in, best, peaks,
    vis_sem, pair_send, pair_recv, col_send, col_recv, row_send, row_recv,
    relay_send, relay_recv, peak_send, peak_recv,
    ) = scratch
    copies = [
        pltpu.make_async_copy(source, target, small_sem.at[n])
        for n, (source, target) in enumerate(zip(small, scratch[:5]))
    ]
    for copy in copies:
        copy.start()
    m = vis.shape[1]
    width = m // HALVES
    group = FR // GROUPS
    chips = cols // 2
    block_cols = FS // rows
    me_col = lax.axis_index("col")
    me_row = lax.axis_index("row")
    core = lax.rem(me_col, 2)
    chip = me_col // 2
    partner = chip * 2 + 1 - core
    inner = (me_row >= 1) & (me_row <= rows - 2)
    outer = (me_row == 0) | (me_row == rows - 1)
    helps = (me_row == 1) | (me_row == rows - 2)
    end_row = jnp.where(me_row <= 1, 0, rows - 1)
    helper = jnp.where(me_row <= 1, 1, rows - 2)

    def peer_chip(d):
        return lax.rem(chip + d, chips) * 2 + core

    def peer_row(d):
        return lax.rem(me_row + d, rows)

    barrier = pltpu.get_barrier_semaphore()
    pl.semaphore_signal(barrier, inc=1, device_id=(partner, me_row), device_id_type=MESH)
    for d in range(1, chips):
        pl.semaphore_signal(barrier, inc=1, device_id=(peer_chip(d), me_row), device_id_type=MESH)
    for d in range(1, rows):
        pl.semaphore_signal(barrier, inc=1, device_id=(me_col, peer_row(d)), device_id_type=MESH)

    def vis_copy(h, ri):
        part = pl.ds(h * width, width)
        return pltpu.make_async_copy(vis_hbm.at[ri, :, part], vis.at[ri, :, part], vis_sem.at[h, ri])

    for h in range(HALVES):
        for ri in range(2):
            vis_copy(h, ri).start()

    with jax.named_scope("small"):
        for copy in copies:
            copy.wait()

    u = iota((cols, m), 1)
    slot = iota((cols, m), 0)
    start = jnp.zeros((cols, m), jnp.int32)
    for half in range(2):
        for c in range(chips):
            facet = facet_order[c * 2 + (core if half == 0 else 1 - core)]
            first = (facet_off[0, facet] + (FS // 2 - FR // 2)) & (NG - 1)
            start = jnp.where(slot == half * chips + c, first, start)
    real, imag = cis(start * (col_off[0] + u))
    scale = jnp.where(u < counts[0, 0], 1.0 / math.sqrt(m * cols), 0.0)
    head[0] = real * scale
    head[1] = imag * scale
    real, imag = cis(iota((FR, m), 0) * (col_off[0] + iota((FR, m), 1)))
    fine[0] = real
    fine[1] = imag
    block = cols * group
    dot = functools.partial(jnp.dot, preferred_element_type=F32)

    def column_table(g):
        for s in range(cols):
            a, b = head[0, pl.ds(s, 1), :], head[1, pl.ds(s, 1), :]
            c, d = fine[0, pl.ds(g * group, group), :], fine[1, pl.ds(g * group, group), :]
            imag = a * d + b * c
            table[g, pl.ds(s * group, group), :] = (-imag).astype(BF16)
            table[g, pl.ds(block + s * group, group), :] = (a * c - b * d).astype(BF16)
            table[g, pl.ds(2 * block + s * group, group), :] = imag.astype(BF16)

    def pair_copy(n):
        return pltpu.make_async_remote_copy(
            src_ref=pair_out.at[n], dst_ref=pair_in.at[n],
            send_sem=pair_send.at[n], recv_sem=pair_recv.at[n],
            device_id=(partner, me_row), device_id_type=MESH)

    def col_copy(n, d):
        target = lax.rem(chip + d, chips)
        return pltpu.make_async_remote_copy(
            src_ref=sums.at[n, target], dst_ref=others.at[n, d - 1],
            send_sem=col_send.at[n, d - 1], recv_sem=col_recv.at[n, d - 1],
            device_id=(target * 2 + core, me_row), device_id_type=MESH)

    def row_copy(n, origin, target):
        return pltpu.make_async_remote_copy(
            src_ref=gathered.at[n, origin], dst_ref=gathered.at[n, origin],
            send_sem=row_send.at[n, target], recv_sem=row_recv.at[n, origin],
            device_id=(me_col, target), device_id_type=MESH)

    def relay_copy(g, target):
        return pltpu.make_async_remote_copy(
            src_ref=relay_out.at[g], dst_ref=relay_in.at[g],
            send_sem=relay_send.at[g], recv_sem=relay_recv.at[g],
            device_id=(me_col, target), device_id_type=MESH)

    def peak_copy(origin, target):
        return pltpu.make_async_remote_copy(
            src_ref=peaks.at[origin], dst_ref=peaks.at[origin],
            send_sem=peak_send.at[target], recv_sem=peak_recv.at[origin],
            device_id=(me_col, target), device_id_type=MESH)

    def each_inner_row(act):
        for dist in range(rows - 1, 0, -1):
            for step in (dist, -dist):
                target = me_row + step

                @pl.when((target >= 1) & (target <= rows - 2))
                def _():
                    act(target)

    def transform(n):
        g, h = n // HALVES, n % HALVES
        if g == 0:
            vis_copy(h, 0).wait()
            vis_copy(h, 1).wait()
        part = pl.ds(h * width, width)
        both = dot(table[g, pl.ds(block, 2 * block), :], vis[0, :, part])
        both += dot(table[g, pl.ds(0, 2 * block), :], vis[1, :, part])
        both = both.reshape(2, 2, chips, group, width)
        for ri in range(2):
            pair_out[n, :, pl.ds(ri * group, group), :] = both[ri, 1].astype(BF16)
            mine[n, :, pl.ds(ri * group, group), :] = both[ri, 0]

    def pair_sum(n):
        pair_copy(n).wait_recv()
        sums[n] = (mine[n] + pair_in[n].astype(F32)).astype(BF16)
        for d in range(chips - 1, 0, -1):
            col_copy(n, d).start()

    def facet_sum(n):
        total = mine[n, chip] + pair_in[n, chip].astype(F32)
        for d in range(1, chips):
            col_copy(n, d).wait_recv()
            total = total + others[n, d - 1].astype(F32)
        gathered[n, me_row] = total.astype(BF16)
        each_inner_row(lambda target: row_copy(n, me_row, target).start())

    def row_table(at, block_row):
        column0 = (facet_off[1, facet_order[me_col]] + block_row * block_cols) & (NG - 1)
        shape = (m // FINE, block_cols)
        real, imag = cis(iota(shape, 0) * FINE * (column0 + iota(shape, 1)))
        coarse2[0] = real
        coarse2[1] = imag
        shape = (FINE, block_cols)
        real, imag = cis(iota(shape, 0) * (column0 + iota(shape, 1)))
        fine2[0] = real
        fine2[1] = imag

        def fill(h, carry):
            a, b = coarse2[0, pl.ds(h, 1), :], coarse2[1, pl.ds(h, 1), :]
            c, d = fine2[0], fine2[1]
            out = pl.ds(pl.multiple_of(h * FINE, FINE), FINE)
            table2[at, 0, out, :] = (a * c - b * d).astype(BF16)
            table2[at, 1, out, :] = (a * d + b * c).astype(BF16)
            return carry

        lax.fori_loop(0, m // FINE, fill, 0)
        row_ids = iota((rows, block_cols), 0)
        offsets = jnp.zeros((rows, block_cols), jnp.int32)
        for r in range(rows):
            offsets = jnp.where(row_ids == r, row_off[r], offsets)
        lanes = iota((rows, block_cols), 1)
        beam = 1.0 - BEAM_SLOPE * ((block_row * block_cols + lanes).astype(F32) + 0.5) / FS
        gain = (0.5 / math.sqrt(m * rows)) / beam
        real, imag = cis(offsets * ((column0 + lanes) & (NG - 1)))
        phases[at, 0] = real * gain
        phases[at, 1] = imag * gain

    piece = min(512, block_cols)

    def second(g, at):
        strongest = best[...]
        for c0 in range(0, block_cols, piece):
            part = pl.ds(c0, piece)
            sides = []
            for side in range(2):
                product = None
                for h in range(HALVES):
                    left = gathered[g * HALVES + h].reshape(rows * 2 * group, width)
                    term = dot(left, table2[at, side, pl.ds(h * width, width), part])
                    product = term if product is None else product + term
                sides.append(product.reshape(rows, 2, group, piece))
            out_real = jnp.zeros((group, piece), F32)
            out_imag = jnp.zeros((group, piece), F32)
            for r in range(rows):
                real = sides[0][r, 0] - sides[1][r, 1]
                imag = sides[1][r, 0] + sides[0][r, 1]
                a, b = phases[at, 0, pl.ds(r, 1), part], phases[at, 1, pl.ds(r, 1), part]
                out_real = out_real + (real * a - imag * b)
                out_imag = out_imag + (real * b + imag * a)
            if at == 0:
                image[0, 0, pl.ds(g * group, group), part] = out_real
                image[0, 1, pl.ds(g * group, group), part] = out_imag
            else:
                relay_out[g, pl.ds(0, group), part] = out_real.astype(BF16)
                relay_out[g, pl.ds(group, group), part] = out_imag.astype(BF16)
            power = out_real * out_real + out_imag * out_imag
            power = jnp.max(power.reshape(group // 8, 8, piece), axis=0)
            for lane in range(0, piece, 128):
                strongest = jnp.maximum(strongest, power[:, lane : lane + 128])
        best[...] = strongest

    def row_group(g):
        for h in range(HALVES):
            for origin in range(rows):
                @pl.when(me_row != origin)
                def _():
                    row_copy(g * HALVES + h, origin, origin).wait_recv()

        @pl.when(helps)
        def _():
            second(g, 1)
            relay_copy(g, end_row).start()

        second(g, 0)

    best[...] = jnp.zeros(best.shape, F32)
    for n in range(CHUNKS):
        if n % HALVES == 0:
            with jax.named_scope(f"table{n}"):
                column_table(n // HALVES)
        with jax.named_scope(f"tr{n}"):
            transform(n)
        with jax.named_scope(f"send{n}"):
            if n == 0:
                pl.semaphore_wait(barrier, chips + rows - 1)
            pair_copy(n).start()
        if n > 0:
            with jax.named_scope(f"pair{n - 1}"):
                pair_sum(n - 1)
    with jax.named_scope("pairlast"):
        pair_sum(CHUNKS - 1)

    for n in range(CHUNKS):
        with jax.named_scope(f"facet{n}"):
            facet_sum(n)
        if n == 0:
            @pl.when(inner)
            def _():
                with jax.named_scope("rowtab0"):
                    row_table(0, me_row)
        if n == 1:
            @pl.when(helps)
            def _():
                with jax.named_scope("rowtab1"):
                    row_table(1, end_row)
        ready = n - HALVES - 2
        if ready >= 0 and ready % HALVES == 0 and n < CHUNKS - 1:
            @pl.when(inner)
            def _():
                with jax.named_scope(f"group{ready // HALVES}"):
                    row_group(ready // HALVES)
    for g in range((CHUNKS - 2 - HALVES - 2) // HALVES + 1, GROUPS):
        @pl.when(inner)
        def _():
            with jax.named_scope(f"group{g}"):
                row_group(g)

    @pl.when(inner)
    def _():
        peaks[me_row] = jnp.sqrt(best[...])
        for d in range(1, rows):
            peak_copy(me_row, peer_row(d)).start()

    @pl.when(outer)
    def _():
        for g in range(GROUPS):
            with jax.named_scope(f"relay{g}"):
                relay_copy(g, helper).wait_recv()
                for ri in range(2):
                    image[0, ri, pl.ds(g * group, group), :] = relay_in[g, pl.ds(ri * group, group), :].astype(F32)

    with jax.named_scope("sends"):
        for n in range(CHUNKS):
            pair_copy(n).wait_send()
            for d in range(1, chips):
                col_copy(n, d).wait_send()
            each_inner_row(lambda target: row_copy(n, me_row, target).wait_send())

        @pl.when(helps)
        def _():
            for g in range(GROUPS):
                relay_copy(g, end_row).wait_send()

    with jax.named_scope("peakwait"):
        for origin in range(1, rows - 1):
            @pl.when(me_row != origin)
            def _():
                peak_copy(origin, origin).wait_recv()

        @pl.when(inner)
        def _():
            for d in range(1, rows):
                peak_copy(me_row, peer_row(d)).wait_send()

        strongest = peaks[1]
        for r in range(2, rows - 1):
            strongest = jnp.maximum(strongest, peaks[r])
        peak[0] = jnp.max(strongest)


def local(cols, rows, visibilities, col_offsets, row_offsets, facet_offsets, facet_order, vis_counts):
    m = visibilities.shape[1]
    width = m // HALVES
    group = FR // GROUPS
    chips = cols // 2
    block_cols = FS // rows
    dma = pltpu.SemaphoreType.DMA
    smem = pl.BlockSpec(memory_space=pltpu.SMEM)
    anywhere = pl.BlockSpec(memory_space=pl.ANY)
    small = (col_offsets, row_offsets, facet_offsets.T, facet_order, vis_counts)
    return pl.pallas_call(
        functools.partial(kernel, cols, rows),
        out_shape=(
            pltpu.VMEM((1, 2, FR, block_cols), F32),
            jax.ShapeDtypeStruct((1,), F32),
        ),
        in_specs=[anywhere] * 6,
        out_specs=(pl.BlockSpec(memory_space=pltpu.VMEM), smem),
        scratch_shapes=[pltpu.SMEM(x.shape, x.dtype) for x in small] + [
            dma((len(small),)),
            pltpu.VMEM((2, m, m), BF16),
            pltpu.VMEM((2, cols, m), F32),
            pltpu.VMEM((2, FR, m), F32),
            pltpu.VMEM((GROUPS, 3 * cols * group, m), BF16),
            pltpu.VMEM((CHUNKS, chips, 2 * group, width), F32),
            pltpu.VMEM((CHUNKS, chips, 2 * group, width), BF16),
            pltpu.VMEM((CHUNKS, chips, 2 * group, width), BF16),
            pltpu.VMEM((CHUNKS, chips, 2 * group, width), BF16),
            pltpu.VMEM((CHUNKS, chips - 1, 2 * group, width), BF16),
            pltpu.VMEM((CHUNKS, rows, 2 * group, width), BF16),
            pltpu.VMEM((2, m // FINE, block_cols), F32),
            pltpu.VMEM((2, FINE, block_cols), F32),
            pltpu.VMEM((2, 2, m, block_cols), BF16),
            pltpu.VMEM((2, 2, rows, block_cols), F32),
            pltpu.VMEM((GROUPS, 2 * group, block_cols), BF16),
            pltpu.VMEM((GROUPS, 2 * group, block_cols), BF16),
            pltpu.VMEM((8, 128), F32),
            pltpu.VMEM((rows, 8, 128), F32),
            dma((HALVES, 2)),
            dma((CHUNKS,)),
            dma((CHUNKS,)),
            dma((CHUNKS, chips - 1)),
            dma((CHUNKS, chips - 1)),
            dma((CHUNKS, rows)),
            dma((CHUNKS, rows)),
            dma((GROUPS,)),
            dma((GROUPS,)),
            dma((rows,)),
            dma((rows,)),
        ],
        compiler_params=pltpu.CompilerParams(
            collective_id=0, has_side_effects=True, vmem_limit_bytes=60 * 1024 * 1024),
    )(visibilities, *small)


def solution(mesh):
    in_specs = (P(None, "col", "row"), P("col"), P(), P(), P(), P("col", "row"))
    out_specs = (P("col", None, None, "row"), P("col"))
    body = functools.partial(local, mesh.shape["col"], mesh.shape["row"])
    return jax.shard_map(body, mesh=mesh, in_specs=in_specs, out_specs=out_specs, check_vma=False)
```

time: 44.4 us -> 37.4 us (0.84)
  Pallas kernels: 39.8 us -> 32.8 us
    pallas_call x1, Pallas kernels: 39.8 us -> 32.8 us  [local(): pl.pallas_call(functools.partial(kernel, cols, rows), out_shape=(pltpu.VM...]
where the time goes in v1:
time: 37.4 us; the launch traced here: 37.2 us
  Pallas kernels  32.8 us (88%)
  between operations  3.62 us (10%)
  local copies, waits for them, and re-layouts  0.8 us (2%)
    pallas_call x1, Pallas kernels, local(): pl.pallas_call(functools.partial(kernel, cols, rows), out_shape=(pltpu.VM...  32.8 us
    unnamed x1, local copies, waits for them, and re-layouts  0.8 us

profile of v1, /device:TPU:0, one launch (start us, length us, event | category | flops | bytes accessed | tf_op | source)
XLA Modules:
  0.0 37.2 jit_solution(17448036866788334504)
XLA Ops:
  1.9 32.8 %shard_map.77 = (f32[1,2,64,1024]{3,2,1,0:T(8,128)S(1)}, f32[1]{0:T(128)}) custom-call(bf16[2,1024,1024]{2,1,0:T(8,128)(2,1)} %vis_hbm.1, s32[1]{0:T(128)S(6)} %copy.11.refs_0_, s32[4]{0:T(128)} %refs_1_.1, s32[2,8]{1,0:T(2,128)} %bitcast.1, s32[8]{0:T(128)} %refs_3_.1, s32[1,1]{1,0:T(1,128)S(6)} %copy.12.refs_4_), custom_call_target="tpu_custom_call" | custom-call | tf_op jit(solution)/shard_map/pallas_call | solution.py:373
  34.7 0.8 %copy.10 = f32[1,2,64,1024]{3,2,1,0:T(8,128)} copy(f32[1,2,64,1024]{3,2,1,0:T(8,128)S(1)} %get-tuple-element.2) | data formatting | bytes 1048576

commit v2 on v1

v2 whole, which is shorter than its diff:
```python
import functools
import math

import jax
import jax.numpy as jnp
from jax import lax
from jax.experimental import pallas as pl
from jax.experimental.pallas import tpu as pltpu
from jax.sharding import PartitionSpec as P

FS = 4096
NG = 16384
FR = 64
TWO_PI = 2.0 * math.pi
BEAM_SLOPE = 0.66
FINE = 32
GROUPS = 4
ORDER = (
    "T0 T1 R0 P0 T2 P1 T3 P2 T4 P3 T5 P4 T6 P5 F0 T7 P6 F1 T8 P7 T9 P8 F2 P9 B0 F3 B1 B2",
    "F4 B3 R1 B4 F5 B5 B6 B7 F6 E0 F7 S0 F8 F9 E1 S1 E2 S2 E3 S3",
)
MESH = pl.DeviceIdType.MESH
F32 = jnp.float32
BF16 = jnp.bfloat16


def cis(product):
    shift = (NG // 4).bit_length() - 1
    turn = product & (NG - 1)
    quadrant = (turn + NG // 8) >> shift
    rest = turn - (quadrant << shift)
    angle = rest.astype(F32) * (TWO_PI / NG)
    z = angle * angle
    sine = angle * (1.0 + z * (-1.0 / 6 + z * (1.0 / 120 + z * (-1.0 / 5040 + z * (1.0 / 362880)))))
    cosine = 1.0 + z * (-0.5 + z * (1.0 / 24 + z * (-1.0 / 720 + z * (1.0 / 40320))))
    odd = (quadrant & 1) == 1
    real = jnp.where(odd, sine, cosine)
    imag = jnp.where(odd, cosine, sine)
    real = jnp.where(((quadrant + 1) & 2) != 0, -real, real)
    imag = jnp.where((quadrant & 2) != 0, -imag, imag)
    return real, imag


def iota(shape, dim):
    return lax.broadcasted_iota(jnp.int32, shape, dim)


def chunk_plan(m):
    half, quarter = m // 2, m // 4
    plan = []
    for g in range(GROUPS):
        for h in range(2):
            if (g, h) in ((0, 0), (GROUPS - 1, 1)):
                plan += [(g, h * half, quarter), (g, h * half + quarter, quarter)]
            else:
                plan.append((g, h * half, half))
    return plan


def kernel(
    cols, rows, plan,
    vis_hbm, *refs,
):
    small, (image, peak), scratch = refs[:5], refs[5:7], refs[7:]
    (
    col_off, row_off, facet_off, facet_order, counts, small_sem,
    vis, head, fine, table, mine, pair_out, pair_in, sums, others, gathered,
    coarse2, fine2, table2, phases, relay_out, relay_in, best, peaks,
    vis_sem, pair_send, pair_recv, col_send, col_recv, row_send, row_recv,
    relay_send, relay_recv, peak_send, peak_recv,
    ) = scratch
    copies = [
        pltpu.make_async_copy(source, target, small_sem.at[n])
        for n, (source, target) in enumerate(zip(small, scratch[:5]))
    ]
    for copy in copies:
        copy.start()
    m = vis.shape[1]
    group = FR // GROUPS
    chips = cols // 2
    block_cols = FS // rows
    piece = min(512, block_cols)
    chunks = len(plan)
    me_col = lax.axis_index("col")
    me_row = lax.axis_index("row")
    core = lax.rem(me_col, 2)
    chip = me_col // 2
    partner = chip * 2 + 1 - core
    inner = (me_row >= 1) & (me_row <= rows - 2)
    outer = (me_row == 0) | (me_row == rows - 1)
    helps = (me_row == 1) | (me_row == rows - 2)
    end_row = jnp.where(me_row <= 1, 0, rows - 1)

    def peer_chip(d):
        return lax.rem(chip + d, chips) * 2 + core

    def peer_row(d):
        return lax.rem(me_row + d, rows)

    barrier = pltpu.get_barrier_semaphore()
    pl.semaphore_signal(barrier, inc=1, device_id=(partner, me_row), device_id_type=MESH)
    for d in range(1, chips):
        pl.semaphore_signal(barrier, inc=1, device_id=(peer_chip(d), me_row), device_id_type=MESH)
    for d in range(1, rows):
        pl.semaphore_signal(barrier, inc=1, device_id=(me_col, peer_row(d)), device_id_type=MESH)

    strips = [(v0, width) for g, v0, width in plan if g == 0]

    def vis_copy(h):
        part = pl.ds(*strips[h])
        return pltpu.make_async_copy(vis_hbm.at[:, :, part], vis.at[:, :, part], vis_sem.at[h])

    for h in range(len(strips)):
        vis_copy(h).start()

    real, imag = cis(iota((FR, m), 0) * iota((FR, m), 1))
    fine[0] = real
    fine[1] = imag
    best[...] = jnp.zeros(best.shape, F32)

    with jax.named_scope("small"):
        for copy in copies:
            copy.wait()

    u = iota((cols, m), 1)
    slot = iota((cols, m), 0)
    start = jnp.zeros((cols, m), jnp.int32)
    for half in range(2):
        for c in range(chips):
            facet = facet_order[c * 2 + (core if half == 0 else 1 - core)]
            first = (facet_off[0, facet] + (FS // 2 - FR // 2)) & (NG - 1)
            start = jnp.where(slot == half * chips + c, first, start)
    real, imag = cis(start * (col_off[0] + u))
    scale = jnp.where(u < counts[0, 0], 1.0 / math.sqrt(m * cols), 0.0)
    head[0] = real * scale
    head[1] = imag * scale
    turns = cis(iota((FR, 128), 0) * col_off[0])
    block = cols * group
    dot = functools.partial(jnp.dot, preferred_element_type=F32)

    def column_table(g):
        rows_here = slice(g * group, (g + 1) * group)
        a, b = (jnp.concatenate([x[rows_here]] * (m // 128), axis=1) for x in turns)
        c, d = fine[0, rows_here, :], fine[1, rows_here, :]
        c, d = a * c - b * d, a * d + b * c
        for s in range(cols):
            a, b = head[0, pl.ds(s, 1), :], head[1, pl.ds(s, 1), :]
            imag = a * d + b * c
            real = a * c - b * d
            table[g, pl.ds(s * group, group), :] = real.astype(BF16)
            table[g, pl.ds(block + s * group, group), :] = imag.astype(BF16)
            table[g, pl.ds(2 * block + s * group, group), :] = (-real).astype(BF16)

    def pair_copy(n):
        g, v0, width = plan[n]
        part = pl.ds(v0, width)
        return pltpu.make_async_remote_copy(
            src_ref=pair_out.at[g, :, :, part], dst_ref=pair_in.at[g, :, :, part],
            send_sem=pair_send, recv_sem=pair_recv.at[n],
            device_id=(partner, me_row), device_id_type=MESH)

    def col_copy(n, d):
        g, v0, width = plan[n]
        part = pl.ds(v0, width)
        target = lax.rem(chip + d, chips)
        return pltpu.make_async_remote_copy(
            src_ref=sums.at[g, target, :, part], dst_ref=others.at[g, d - 1, :, part],
            send_sem=col_send, recv_sem=col_recv.at[n],
            device_id=(target * 2 + core, me_row), device_id_type=MESH)

    def row_copy(n, target):
        g, v0, width = plan[n]
        part = pl.ds(v0, width)
        return pltpu.make_async_remote_copy(
            src_ref=gathered.at[g, me_row, :, part], dst_ref=gathered.at[g, me_row, :, part],
            send_sem=row_send, recv_sem=row_recv.at[g],
            device_id=(me_col, target), device_id_type=MESH)

    def relay_copy(g, p):
        return pltpu.make_async_remote_copy(
            src_ref=relay_out.at[g, p], dst_ref=relay_in.at[g, p],
            send_sem=relay_send, recv_sem=relay_recv.at[g],
            device_id=(me_col, end_row), device_id_type=MESH)

    def peak_copy(target):
        return pltpu.make_async_remote_copy(
            src_ref=peaks.at[me_row], dst_ref=peaks.at[me_row],
            send_sem=peak_send, recv_sem=peak_recv,
            device_id=(me_col, target), device_id_type=MESH)

    def wait_bytes(ref, sem):
        pltpu.make_async_copy(ref, ref, sem).wait()

    def each_inner_row(act):
        for dist in range(rows - 1, 0, -1):
            for step in (dist, -dist):
                target = me_row + step

                @pl.when((target >= 1) & (target <= rows - 2))
                def _():
                    act(target)

    def transform(n):
        g, v0, width = plan[n]
        part = pl.ds(v0, width)
        if g == 0:
            vis_copy(n).wait()
        both = dot(table[g, pl.ds(0, 2 * block), :], vis[0, :, part])
        both = both - dot(table[g, pl.ds(block, 2 * block), :], vis[1, :, part])
        both = both.reshape(2, 2, chips, group, width)
        for ri in range(2):
            pair_out[g, :, pl.ds(ri * group, group), part] = both[ri, 1].astype(BF16)
            mine[g, :, pl.ds(ri * group, group), part] = both[ri, 0]

    def pair_sum(n):
        pair_copy(n).wait_recv()
        g, v0, width = plan[n]
        part = pl.ds(v0, width)
        sums[g, :, :, part] = (mine[g, :, :, part] + pair_in[g, :, :, part].astype(F32)).astype(BF16)
        for d in range(chips - 1, 0, -1):
            col_copy(n, d).start()

    def facet_sum(n):
        g, v0, width = plan[n]
        part = pl.ds(v0, width)
        wait_bytes(others.at[g, :, :, part], col_recv.at[n])
        total = mine[g, chip, :, part] + pair_in[g, chip, :, part].astype(F32)
        for d in range(1, chips):
            total = total + others[g, d - 1, :, part].astype(F32)
        gathered[g, me_row, :, part] = total.astype(BF16)
        each_inner_row(lambda target: row_copy(n, target).start())

    def row_start(at, block_row):
        column0 = (facet_off[1, facet_order[me_col]] + block_row * block_cols) & (NG - 1)
        shape = (m // FINE, block_cols)
        real, imag = cis(iota(shape, 0) * FINE * (column0 + iota(shape, 1)))
        coarse2[at, 0] = real
        coarse2[at, 1] = imag
        shape = (FINE, block_cols)
        real, imag = cis(iota(shape, 0) * (column0 + iota(shape, 1)))
        fine2[at, 0] = real
        fine2[at, 1] = imag
        row_ids = iota((rows, block_cols), 0)
        offsets = jnp.zeros((rows, block_cols), jnp.int32)
        for r in range(rows):
            offsets = jnp.where(row_ids == r, row_off[r], offsets)
        lanes = iota((rows, block_cols), 1)
        beam = 1.0 - BEAM_SLOPE * ((block_row * block_cols + lanes).astype(F32) + 0.5) / FS
        gain = (0.5 / math.sqrt(m * rows)) / beam
        real, imag = cis(offsets * ((column0 + lanes) & (NG - 1)))
        phases[at, 0] = real * gain
        phases[at, 1] = imag * gain

    def row_fill(at, first, last):
        def fill(h, carry):
            a, b = coarse2[at, 0, pl.ds(h, 1), :], coarse2[at, 1, pl.ds(h, 1), :]
            c, d = fine2[at, 0], fine2[at, 1]
            out = pl.ds(pl.multiple_of(h * FINE, FINE), FINE)
            table2[at, 0, out, :] = (a * c - b * d).astype(BF16)
            table2[at, 1, out, :] = (a * d + b * c).astype(BF16)
            return carry

        lax.fori_loop(first, last, fill, 0)

    def second(g, at):
        strongest = best[...]
        for p in range(block_cols // piece):
            part = pl.ds(p * piece, piece)
            sides = []
            for side in range(2):
                left = gathered[g].reshape(rows * 2 * group, m)
                product = dot(left, table2[at, side, :, part])
                sides.append(product.reshape(rows, 2, group, piece))
            out_real = jnp.zeros((group, piece), F32)
            out_imag = jnp.zeros((group, piece), F32)
            for r in range(rows):
                real = sides[0][r, 0] - sides[1][r, 1]
                imag = sides[1][r, 0] + sides[0][r, 1]
                a, b = phases[at, 0, pl.ds(r, 1), part], phases[at, 1, pl.ds(r, 1), part]
                out_real = out_real + (real * a - imag * b)
                out_imag = out_imag + (real * b + imag * a)
            if at == 0:
                image[0, 0, pl.ds(g * group, group), part] = out_real
                image[0, 1, pl.ds(g * group, group), part] = out_imag
            else:
                relay_out[g, p, pl.ds(0, group), :] = out_real.astype(BF16)
                relay_out[g, p, pl.ds(group, group), :] = out_imag.astype(BF16)
                relay_copy(g, p).start()
            power = out_real * out_real + out_imag * out_imag
            power = jnp.max(power.reshape(group // 8, 8, piece), axis=0)
            for lane in range(0, piece, 128):
                strongest = jnp.maximum(strongest, power[:, lane : lane + 128])
        best[...] = strongest

    def when(condition, name, act, *args):
        @pl.when(condition)
        def _():
            with jax.named_scope(name):
                act(*args)

    def arrive(g):
        wait_bytes(gathered.at[g, pl.ds(0, rows - 1)], row_recv.at[g])

    def scoped(name, act, *args):
        with jax.named_scope(name):
            act(*args)

    def T(n):
        if plan[n][1] == 0:
            scoped(f"table{n}", column_table, plan[n][0])
        scoped(f"tr{n}", transform, n)
        if n == 0:
            scoped("barrier", pl.semaphore_wait, barrier, chips + rows - 1)
        pair_copy(n).start()

    def P(n):
        scoped(f"pair{n}", pair_sum, n)

    def F(n):
        scoped(f"facet{n}", facet_sum, n)

    def R(at):
        when(inner if at == 0 else helps, f"start{at}", row_start, at, me_row if at == 0 else end_row)

    def B(step):
        at, quarter = step // 4, step % 4
        fills = m // FINE // 4
        when(inner if at == 0 else helps, f"fill{step}", row_fill, at, quarter * fills, (quarter + 1) * fills)

    def E(g):
        when(inner, f"arrive{g}", arrive, g)
        when(helps, f"second{g}1", second, g, 1)

    def S(g):
        when(inner, f"second{g}0", second, g, 0)

    steps = {"T": T, "P": P, "F": F, "R": R, "B": B, "E": E, "S": S}
    for part in ORDER:
        for step in part.split():
            steps[step[0]](int(step[1:]))

    @pl.when(inner)
    def _():
        peaks[me_row] = jnp.sqrt(best[...])
        for d in range(1, rows):
            peak_copy(peer_row(d)).start()

    @pl.when(outer)
    def _():
        for g in range(GROUPS):
            with jax.named_scope(f"relay{g}"):
                wait_bytes(relay_in.at[g], relay_recv.at[g])
                for p in range(block_cols // piece):
                    for ri in range(2):
                        here = relay_in[g, p, pl.ds(ri * group, group), :]
                        image[0, ri, pl.ds(g * group, group), pl.ds(p * piece, piece)] = here.astype(F32)

    with jax.named_scope("sends"):
        wait_bytes(pair_out, pair_send)
        wait_bytes(others, col_send)

        @pl.when(outer)
        def _():
            wait_bytes(gathered.at[:, pl.ds(0, rows - 2)], row_send)

        @pl.when(inner)
        def _():
            wait_bytes(gathered.at[:, pl.ds(0, rows - 3)], row_send)

        @pl.when(helps)
        def _():
            wait_bytes(relay_out, relay_send)

    with jax.named_scope("peakwait"):
        @pl.when(outer)
        def _():
            wait_bytes(peaks.at[pl.ds(0, rows - 2)], peak_recv)

        @pl.when(inner)
        def _():
            wait_bytes(peaks.at[pl.ds(0, rows - 3)], peak_recv)
            wait_bytes(peaks.at[pl.ds(0, rows - 1)], peak_send)

        strongest = peaks[1]
        for r in range(2, rows - 1):
            strongest = jnp.maximum(strongest, peaks[r])
        peak[0] = jnp.max(strongest)


def local(cols, rows, visibilities, col_offsets, row_offsets, facet_offsets, facet_order, vis_counts):
    m = visibilities.shape[1]
    plan = chunk_plan(m)
    chunks = len(plan)
    strips = sum(g == 0 for g, _, _ in plan)
    group = FR // GROUPS
    chips = cols // 2
    block_cols = FS // rows
    piece = min(512, block_cols)

    def blocks(lead, dtype):
        return pltpu.VMEM((GROUPS, lead, 2 * group, m), dtype)

    dma = pltpu.SemaphoreType.DMA
    smem = pl.BlockSpec(memory_space=pltpu.SMEM)
    anywhere = pl.BlockSpec(memory_space=pl.ANY)
    small = (col_offsets, row_offsets, facet_offsets.T, facet_order, vis_counts)
    return pl.pallas_call(
        functools.partial(kernel, cols, rows, plan),
        out_shape=(
            pltpu.VMEM((1, 2, FR, block_cols), F32),
            pltpu.SMEM((1,), F32),
        ),
        in_specs=[anywhere] * 6,
        out_specs=(pl.BlockSpec(memory_space=pltpu.VMEM), smem),
        scratch_shapes=[pltpu.SMEM(x.shape, x.dtype) for x in small] + [
            dma((len(small),)),
            pltpu.VMEM((2, m, m), BF16),
            pltpu.VMEM((2, cols, m), F32),
            pltpu.VMEM((2, FR, m), F32),
            pltpu.VMEM((GROUPS, 3 * cols * group, m), BF16),
            blocks(chips, F32),
            blocks(chips, BF16),
            blocks(chips, BF16),
            blocks(chips, BF16),
            blocks(chips - 1, BF16),
            blocks(rows, BF16),
            pltpu.VMEM((2, 2, m // FINE, block_cols), F32),
            pltpu.VMEM((2, 2, FINE, block_cols), F32),
            pltpu.VMEM((2, 2, m, block_cols), BF16),
            pltpu.VMEM((2, 2, rows, block_cols), F32),
            pltpu.VMEM((GROUPS, block_cols // piece, 2 * group, piece), BF16),
            pltpu.VMEM((GROUPS, block_cols // piece, 2 * group, piece), BF16),
            pltpu.VMEM((8, 128), F32),
            pltpu.VMEM((rows, 8, 128), F32),
            dma((strips,)),
            dma,
            dma((chunks,)),
            dma,
            dma((chunks,)),
            dma,
            dma((GROUPS,)),
            dma,
            dma((GROUPS,)),
            dma,
            dma,
        ],
        compiler_params=pltpu.CompilerParams(
            collective_id=0, has_side_effects=True, vmem_limit_bytes=60 * 1024 * 1024),
    )(visibilities, *small)


def solution(mesh):
    in_specs = (P(None, "col", "row"), P("col"), P(), P(), P(), P("col", "row"))
    out_specs = (P("col", None, None, "row"), P("col"))
    body = functools.partial(local, mesh.shape["col"], mesh.shape["row"])
    return jax.shard_map(body, mesh=mesh, in_specs=in_specs, out_specs=out_specs, check_vma=False)
```

time: 37.4 us -> 34.5 us (0.922)
  Pallas kernels: 32.8 us -> 31 us
  between operations: 3.62 us -> 2.45 us
    pallas_call x1, Pallas kernels: 32.8 us -> 31 us  [local(): pl.pallas_call(functools.partial(kernel, cols, rows, plan), out_shape=(pl...]
where the time goes in v2:
time: 34.5 us; the launch traced here: 34.3 us
  Pallas kernels  31 us (90%)
  between operations  2.45 us (7%)
  local copies, waits for them, and re-layouts  0.8 us (2%)
    pallas_call x1, Pallas kernels, local(): pl.pallas_call(functools.partial(kernel, cols, rows, plan), out_shape=(pl...  31 us
    unnamed x1, local copies, waits for them, and re-layouts  0.8 us

profile of v2, /device:TPU:0, one launch (start us, length us, event | category | flops | bytes accessed | tf_op | source)
XLA Modules:
  0.0 34.3 jit_solution(3560489326127177863)
XLA Ops:
  1.9 31.0 %shard_map.77 = (f32[1,2,64,1024]{3,2,1,0:T(8,128)S(1)}, f32[1]{0:T(128)S(4)}) custom-call(bf16[2,1024,1024]{2,1,0:T(8,128)(2,1)} %vis_hbm.1, s32[1]{0:T(128)S(6)} %copy.12.refs_0_, s32[4]{0:T(128)} %refs_1_.1, s32[2,8]{1,0:T(2,128)} %bitcast.1, s32[8]{0:T(128)} %refs_3_.1, s32[1,1]{1,0:T(1,128)S(6)} %copy.13.refs_4_), custom_call_target="tpu_custom_call" | custom-call | tf_op jit(solution)/shard_map/pallas_call | solution.py:407
  33.5 0.8 %copy.10 = f32[1,2,64,1024]{3,2,1,0:T(8,128)} copy(f32[1,2,64,1024]{3,2,1,0:T(8,128)S(1)} %get-tuple-element.2) | data formatting | bytes 1048576

commit v3 on v2

--- a/solution.py
+++ b/solution.py
@@ -16,8 +16,10 @@
 FINE = 32
 GROUPS = 4
 ORDER = (
-    "T0 T1 R0 P0 T2 P1 T3 P2 T4 P3 T5 P4 T6 P5 F0 T7 P6 F1 T8 P7 T9 P8 F2 P9 B0 F3 B1 B2",
-    "F4 B3 R1 B4 F5 B5 B6 B7 F6 E0 F7 S0 F8 F9 E1 S1 E2 S2 E3 S3",
+    "T0", "T1", "R0", "P0", "N0", "T2", "P1", "N1", "T3", "B0", "B1", "P2", "T4", "P3", "N2", "T5", "P4", "N3",
+    "F0", "T6", "F1", "P5", "N4", "T7", "F2", "T8", "P6", "N5", "B2", "B3", "F3", "T9", "P7", "N6", "P8", "N7",
+    "R1", "B4", "F4", "P9", "N8", "N9", "B5", "B6", "B7", "F5", "E0", "F6", "S0", "F7", "E1", "F8", "F9", "S1",
+    "E2", "S2", "H0", "H1", "E3", "S3",
 )
 MESH = pl.DeviceIdType.MESH
 F32 = jnp.float32
@@ -65,7 +67,7 @@
     (
     col_off, row_off, facet_off, facet_order, counts, small_sem,
     vis, head, fine, table, mine, pair_out, pair_in, sums, others, gathered,
-    coarse2, fine2, table2, phases, relay_out, relay_in, best, peaks,
+    coarse2, fine2, table2, phases, relay_out, relay_in, early, best, peaks,
     vis_sem, pair_send, pair_recv, col_send, col_recv, row_send, row_recv,
     relay_send, relay_recv, peak_send, peak_recv,
     ) = scratch
@@ -102,7 +104,9 @@
     for d in range(1, chips):
         pl.semaphore_signal(barrier, inc=1, device_id=(peer_chip(d), me_row), device_id_type=MESH)
     for d in range(1, rows):
-        pl.semaphore_signal(barrier, inc=1, device_id=(me_col, peer_row(d)), device_id_type=MESH)
+        @pl.when(inner | ((peer_row(d) >= 1) & (peer_row(d) <= rows - 2)))
+        def _():
+            pl.semaphore_signal(barrier, inc=1, device_id=(me_col, peer_row(d)), device_id_type=MESH)
 
     strips = [(v0, width) for g, v0, width in plan if g == 0]
 
@@ -159,12 +163,11 @@
             send_sem=pair_send, recv_sem=pair_recv.at[n],
             device_id=(partner, me_row), device_id_type=MESH)
 
-    def col_copy(n, d):
-        g, v0, width = plan[n]
-        part = pl.ds(v0, width)
-        target = lax.rem(chip + d, chips)
+    def col_copy(n, target):
+        g, v0, width = plan[n]
+        part = pl.ds(v0, width)
         return pltpu.make_async_remote_copy(
-            src_ref=sums.at[g, target, :, part], dst_ref=others.at[g, d - 1, :, part],
+            src_ref=sums.at[g, target, :, part], dst_ref=others.at[g, chip, :, part],
             send_sem=col_send, recv_sem=col_recv.at[n],
             device_id=(target * 2 + core, me_row), device_id_type=MESH)
 
@@ -173,7 +176,7 @@
         part = pl.ds(v0, width)
         return pltpu.make_async_remote_copy(
             src_ref=gathered.at[g, me_row, :, part], dst_ref=gathered.at[g, me_row, :, part],
-            send_sem=row_send, recv_sem=row_recv.at[g],
+            send_sem=row_send, recv_sem=row_recv.at[g + (g == GROUPS - 1 and v0 >= m // 2)],
             device_id=(me_col, target), device_id_type=MESH)
 
     def relay_copy(g, p):
@@ -217,16 +220,20 @@
         g, v0, width = plan[n]
         part = pl.ds(v0, width)
         sums[g, :, :, part] = (mine[g, :, :, part] + pair_in[g, :, :, part].astype(F32)).astype(BF16)
-        for d in range(chips - 1, 0, -1):
-            col_copy(n, d).start()
+
+    def col_start(n):
+        for target in range(chips):
+            @pl.when(target != chip)
+            def _():
+                col_copy(n, target).start()
 
     def facet_sum(n):
         g, v0, width = plan[n]
         part = pl.ds(v0, width)
-        wait_bytes(others.at[g, :, :, part], col_recv.at[n])
+        wait_bytes(others.at[g, pl.ds(0, chips - 1), :, part], col_recv.at[n])
         total = mine[g, chip, :, part] + pair_in[g, chip, :, part].astype(F32)
         for d in range(1, chips):
-            total = total + others[g, d - 1, :, part].astype(F32)
+            total = total + others[g, lax.rem(chip + d, chips), :, part].astype(F32)
         gathered[g, me_row, :, part] = total.astype(BF16)
         each_inner_row(lambda target: row_copy(n, target).start())
 
@@ -268,8 +275,11 @@
             part = pl.ds(p * piece, piece)
             sides = []
             for side in range(2):
-                left = gathered[g].reshape(rows * 2 * group, m)
-                product = dot(left, table2[at, side, :, part])
+                v0 = m // 2 if g == GROUPS - 1 else 0
+                left = gathered[g, :, :, pl.ds(v0, m - v0)].reshape(rows * 2 * group, m - v0)
+                product = dot(left, table2[at, side, pl.ds(v0, m - v0), part])
+                if v0:
+                    product = product + early[at, side, :, part]
                 sides.append(product.reshape(rows, 2, group, piece))
             out_real = jnp.zeros((group, piece), F32)
             out_imag = jnp.zeros((group, piece), F32)
@@ -292,6 +302,11 @@
                 strongest = jnp.maximum(strongest, power[:, lane : lane + 128])
         best[...] = strongest
 
+    def first_half(at):
+        left = gathered[GROUPS - 1, :, :, pl.ds(0, m // 2)].reshape(rows * 2 * group, m // 2)
+        for side in range(2):
+            early[at, side] = dot(left, table2[at, side, pl.ds(0, m // 2), :])
+
     def when(condition, name, act, *args):
         @pl.when(condition)
         def _():
@@ -299,7 +314,12 @@
                 act(*args)
 
     def arrive(g):
-        wait_bytes(gathered.at[g, pl.ds(0, rows - 1)], row_recv.at[g])
+        late = g == GROUPS - 1
+        part = pl.ds(m // 2, m // 2) if late else pl.ds(0, m)
+        wait_bytes(gathered.at[g, pl.ds(0, rows - 1), :, part], row_recv.at[g + late])
+
+    def arrive_half():
+        wait_bytes(gathered.at[GROUPS - 1, pl.ds(0, rows - 1), :, pl.ds(0, m // 2)], row_recv.at[GROUPS - 1])
 
     def scoped(name, act, *args):
         with jax.named_scope(name):
@@ -310,11 +330,16 @@
             scoped(f"table{n}", column_table, plan[n][0])
         scoped(f"tr{n}", transform, n)
         if n == 0:
-            scoped("barrier", pl.semaphore_wait, barrier, chips + rows - 1)
+            when(inner, "barrier", pl.semaphore_wait, barrier, chips + rows - 1)
+            when(outer, "barrier", pl.semaphore_wait, barrier, chips + rows - 2)
         pair_copy(n).start()
 
     def P(n):
         scoped(f"pair{n}", pair_sum, n)
+        when(core == 0, f"col{n}", col_start, n)
+
+    def N(n):
+        when(core == 1, f"col{n}", col_start, n)
 
     def F(n):
         scoped(f"facet{n}", facet_sum, n)
@@ -331,13 +356,19 @@
         when(inner, f"arrive{g}", arrive, g)
         when(helps, f"second{g}1", second, g, 1)
 
+    def H(step):
+        if step == 0:
+            when(inner, "arrivehalf", arrive_half)
+            when(helps, "half1", first_half, 1)
+        else:
+            when(inner, "half0", first_half, 0)
+
     def S(g):
         when(inner, f"second{g}0", second, g, 0)
 
-    steps = {"T": T, "P": P, "F": F, "R": R, "B": B, "E": E, "S": S}
-    for part in ORDER:
-        for step in part.split():
-            steps[step[0]](int(step[1:]))
+    steps = {"T": T, "P": P, "N": N, "F": F, "R": R, "B": B, "E": E, "H": H, "S": S}
+    for step in ORDER:
+        steps[step[0]](int(step[1:]))
 
     @pl.when(inner)
     def _():
@@ -357,7 +388,7 @@
 
     with jax.named_scope("sends"):
         wait_bytes(pair_out, pair_send)
-        wait_bytes(others, col_send)
+        wait_bytes(others.at[:, pl.ds(0, chips - 1)], col_send)
 
         @pl.when(outer)
         def _():
@@ -422,7 +453,7 @@
             blocks(chips, BF16),
             blocks(chips, BF16),
             blocks(chips, BF16),
-            blocks(chips - 1, BF16),
+            blocks(chips, BF16),
             blocks(rows, BF16),
             pltpu.VMEM((2, 2, m // FINE, block_cols), F32),
             pltpu.VMEM((2, 2, FINE, block_cols), F32),
@@ -430,6 +461,7 @@
             pltpu.VMEM((2, 2, rows, block_cols), F32),
             pltpu.VMEM((GROUPS, block_cols // piece, 2 * group, piece), BF16),
             pltpu.VMEM((GROUPS, block_cols // piece, 2 * group, piece), BF16),
+            pltpu.VMEM((2, 2, rows * 2 * group, block_cols), F32),
             pltpu.VMEM((8, 128), F32),
             pltpu.VMEM((rows, 8, 128), F32),
             dma((strips,)),
@@ -438,7 +470,7 @@
             dma,
             dma((chunks,)),
             dma,
-            dma((GROUPS,)),
+            dma((GROUPS + 1,)),
             dma,
             dma((GROUPS,)),
             dma,

time: 34.5 us -> 32.7 us (0.948)
  Pallas kernels: 31 us -> 29.3 us
    pallas_call x1, Pallas kernels: 31 us -> 29.3 us  [local(): pl.pallas_call(functools.partial(kernel, cols, rows, plan), out_shape=(pl...]
where the time goes in v3:
time: 32.7 us; the launch traced here: 32.6 us
  Pallas kernels  29.3 us (90%)
  between operations  2.45 us (7%)
  local copies, waits for them, and re-layouts  0.8 us (2%)
    pallas_call x1, Pallas kernels, local(): pl.pallas_call(functools.partial(kernel, cols, rows, plan), out_shape=(pl...  29.3 us
    unnamed x1, local copies, waits for them, and re-layouts  0.8 us

profile of v3, /device:TPU:0, one launch (start us, length us, event | category | flops | bytes accessed | tf_op | source)
XLA Modules:
  0.0 32.6 jit_solution(6191900430713054443)
XLA Ops:
  1.9 29.3 %shard_map.77 = (f32[1,2,64,1024]{3,2,1,0:T(8,128)S(1)}, f32[1]{0:T(128)S(4)}) custom-call(bf16[2,1024,1024]{2,1,0:T(8,128)(2,1)} %vis_hbm.1, s32[1]{0:T(128)S(6)} %copy.12.refs_0_, s32[4]{0:T(128)} %refs_1_.1, s32[2,8]{1,0:T(2,128)} %bitcast.1, s32[8]{0:T(128)} %refs_3_.1, s32[1,1]{1,0:T(1,128)S(6)} %copy.13.refs_4_), custom_call_target="tpu_custom_call" | custom-call | tf_op jit(solution)/shard_map/pallas_call | solution.py:438
  31.8 0.8 %copy.10 = f32[1,2,64,1024]{3,2,1,0:T(8,128)} copy(f32[1,2,64,1024]{3,2,1,0:T(8,128)S(1)} %get-tuple-element.2) | data formatting | bytes 1048576

commit v4 on v3

--- a/solution.py
+++ b/solution.py
@@ -63,11 +63,11 @@
     cols, rows, plan,
     vis_hbm, *refs,
 ):
-    small, (image, peak), scratch = refs[:5], refs[5:7], refs[7:]
+    small, (image, peaks), scratch = refs[:5], refs[5:7], refs[7:]
     (
     col_off, row_off, facet_off, facet_order, counts, small_sem,
     vis, head, fine, table, mine, pair_out, pair_in, sums, others, gathered,
-    coarse2, fine2, table2, phases, relay_out, relay_in, early, best, peaks,
+    coarse2, fine2, table2, phases, relay_out, relay_in, early, best,
     vis_sem, pair_send, pair_recv, col_send, col_recv, row_send, row_recv,
     relay_send, relay_recv, peak_send, peak_recv,
     ) = scratch
@@ -295,12 +295,14 @@
             else:
                 relay_out[g, p, pl.ds(0, group), :] = out_real.astype(BF16)
                 relay_out[g, p, pl.ds(group, group), :] = out_imag.astype(BF16)
-                relay_copy(g, p).start()
             power = out_real * out_real + out_imag * out_imag
             power = jnp.max(power.reshape(group // 8, 8, piece), axis=0)
             for lane in range(0, piece, 128):
                 strongest = jnp.maximum(strongest, power[:, lane : lane + 128])
         best[...] = strongest
+        if at == 1:
+            for p in range(block_cols // piece):
+                relay_copy(g, p).start()
 
     def first_half(at):
         left = gathered[GROUPS - 1, :, :, pl.ds(0, m // 2)].reshape(rows * 2 * group, m // 2)
@@ -412,10 +414,18 @@
             wait_bytes(peaks.at[pl.ds(0, rows - 3)], peak_recv)
             wait_bytes(peaks.at[pl.ds(0, rows - 1)], peak_send)
 
-        strongest = peaks[1]
-        for r in range(2, rows - 1):
-            strongest = jnp.maximum(strongest, peaks[r])
-        peak[0] = jnp.max(strongest)
+
+def finish_kernel(rows, image, peaks, image_out, peak_out, peak, image_sem, peak_sem):
+    copy = pltpu.make_async_copy(image, image_out, image_sem)
+    copy.start()
+    strongest = peaks[1]
+    for r in range(2, rows - 1):
+        strongest = jnp.maximum(strongest, peaks[r])
+    peak[0] = jnp.max(strongest)
+    peak_copy = pltpu.make_async_copy(peak, peak_out, peak_sem)
+    peak_copy.start()
+    peak_copy.wait()
+    copy.wait()
 
 
 def local(cols, rows, visibilities, col_offsets, row_offsets, facet_offsets, facet_order, vis_counts):
@@ -432,17 +442,17 @@
         return pltpu.VMEM((GROUPS, lead, 2 * group, m), dtype)
 
     dma = pltpu.SemaphoreType.DMA
-    smem = pl.BlockSpec(memory_space=pltpu.SMEM)
+    in_vmem = pl.BlockSpec(memory_space=pltpu.VMEM)
     anywhere = pl.BlockSpec(memory_space=pl.ANY)
     small = (col_offsets, row_offsets, facet_offsets.T, facet_order, vis_counts)
-    return pl.pallas_call(
+    image, peaks = pl.pallas_call(
         functools.partial(kernel, cols, rows, plan),
         out_shape=(
             pltpu.VMEM((1, 2, FR, block_cols), F32),
-            pltpu.SMEM((1,), F32),
+            pltpu.VMEM((rows, 8, 128), F32),
         ),
         in_specs=[anywhere] * 6,
-        out_specs=(pl.BlockSpec(memory_space=pltpu.VMEM), smem),
+        out_specs=(in_vmem, in_vmem),
         scratch_shapes=[pltpu.SMEM(x.shape, x.dtype) for x in small] + [
             dma((len(small),)),
             pltpu.VMEM((2, m, m), BF16),
@@ -463,7 +473,6 @@
             pltpu.VMEM((GROUPS, block_cols // piece, 2 * group, piece), BF16),
             pltpu.VMEM((2, 2, rows * 2 * group, block_cols), F32),
             pltpu.VMEM((8, 128), F32),
-            pltpu.VMEM((rows, 8, 128), F32),
             dma((strips,)),
             dma,
             dma((chunks,)),
@@ -479,6 +488,14 @@
         compiler_params=pltpu.CompilerParams(
             collective_id=0, has_side_effects=True, vmem_limit_bytes=60 * 1024 * 1024),
     )(visibilities, *small)
+    return pl.pallas_call(
+        functools.partial(finish_kernel, rows),
+        out_shape=(jax.ShapeDtypeStruct(image.shape, F32), jax.ShapeDtypeStruct((1,), F32)),
+        in_specs=[in_vmem, in_vmem],
+        out_specs=(anywhere, anywhere),
+        scratch_shapes=[pltpu.SMEM((1,), F32), dma, dma],
+        compiler_params=pltpu.CompilerParams(vmem_limit_bytes=1024 * 1024),
+    )(image, peaks)
 
 
 def solution(mesh):

time: 32.7 us -> 32.1 us (0.982)
  local copies, waits for them, and re-layouts: 0.8 us -> 0 us
  Pallas kernels: 29.3 us -> 30 us
  between operations: 2.45 us -> 1.93 us
    pallas_call x0 -> x1, Pallas kernels: none -> 0.81 us  [local(): pl.pallas_call(functools.partial(finish_kernel, rows), out_shape=(jax.Sha...]
    unnamed x1 -> x0, local copies, waits for them, and re-layouts: 0.8 us -> none
where the time goes in v4:
time: 32.1 us; the launch traced here: 31.9 us
  Pallas kernels  30 us (93%)
  between operations  1.93 us (6%)
    pallas_call x1, Pallas kernels, local(): pl.pallas_call(functools.partial(kernel, cols, rows, plan), out_shape=(pl...  29.2 us
    pallas_call x1, Pallas kernels, local(): pl.pallas_call(functools.partial(finish_kernel, rows), out_shape=(jax.Sha...  0.81 us

profile of v4, /device:TPU:0, one launch (start us, length us, event | category | flops | bytes accessed | tf_op | source)
XLA Modules:
  0.0 31.9 jit_solution(9294278084830802770)
XLA Ops:
  1.9 29.2 %shard_map.77 = (f32[1,2,64,1024]{3,2,1,0:T(8,128)S(1)}, f32[4,8,128]{2,1,0:T(8,128)S(1)}) custom-call(bf16[2,1024,1024]{2,1,0:T(8,128)(2,1)} %vis_hbm.1, s32[1]{0:T(128)S(6)} %copy.8.refs_0_, s32[4]{0:T(128)} %refs_1_.1, s32[2,8]{1,0:T(2,128)} %bitcast.1, s32[8]{0:T(128)} %refs_3_.1, s32[1,1]{1,0:T(1,128)S(6)} %copy.9.refs_4_), custom_call_target="tpu_custom_call" | custom-call | tf_op jit(solution)/shard_map/pallas_call | solution.py:448
  31.1 0.8 %shard_map.78 = (f32[1,2,64,1024]{3,2,1,0:T(8,128)}, f32[1]{0:T(128)}) custom-call(f32[1,2,64,1024]{3,2,1,0:T(8,128)S(1)} %get-tuple-element.4.image, f32[4,8,128]{2,1,0:T(8,128)S(1)} %get-tuple-element.5.peaks), custom_call_target="tpu_custom_call" | custom-call | tf_op jit(solution)/shard_map/pallas_call | solution.py:491

commit v5 on v4

--- a/solution.py
+++ b/solution.py
@@ -16,10 +16,9 @@
 FINE = 32
 GROUPS = 4
 ORDER = (
-    "T0", "T1", "R0", "P0", "N0", "T2", "P1", "N1", "T3", "B0", "B1", "P2", "T4", "P3", "N2", "T5", "P4", "N3",
-    "F0", "T6", "F1", "P5", "N4", "T7", "F2", "T8", "P6", "N5", "B2", "B3", "F3", "T9", "P7", "N6", "P8", "N7",
-    "R1", "B4", "F4", "P9", "N8", "N9", "B5", "B6", "B7", "F5", "E0", "F6", "S0", "F7", "E1", "F8", "F9", "S1",
-    "E2", "S2", "H0", "H1", "E3", "S3",
+    "T0", "T1", "R0", "P0", "N0", "T2", "P1", "T3", "P2", "N1", "B0", "B1", "T4", "P3", "N2", "F0", "T5", "P4",
+    "N3", "F1", "T6", "P5", "N4", "B2", "B3", "F2", "T7", "P6", "N5", "R1", "B4", "F3", "P7", "N6", "N7", "B5",
+    "B6", "B7", "F4", "E0", "F5", "S0", "F6", "E1", "F7", "S1", "E2", "S2", "H0", "H1", "E3", "S3",
 )
 MESH = pl.DeviceIdType.MESH
 F32 = jnp.float32
@@ -48,14 +47,11 @@
 
 
 def chunk_plan(m):
-    half, quarter = m // 2, m // 4
+    half = m // 2
     plan = []
     for g in range(GROUPS):
         for h in range(2):
-            if (g, h) in ((0, 0), (GROUPS - 1, 1)):
-                plan += [(g, h * half, quarter), (g, h * half + quarter, quarter)]
-            else:
-                plan.append((g, h * half, half))
+            plan.append((g, h * half, half))
     return plan
 
 

time: 32.1 us -> 31.9 us (level)
  no operation moved by 1% of the time
where the time goes in v5:
time: 31.9 us; the launch traced here: 31.7 us
  Pallas kernels  29.8 us (93%)
  between operations  1.93 us (6%)
    pallas_call x1, Pallas kernels, local(): pl.pallas_call(functools.partial(kernel, cols, rows, plan), out_shape=(pl...  29 us
    pallas_call x1, Pallas kernels, local(): pl.pallas_call(functools.partial(finish_kernel, rows), out_shape=(jax.Sha...  0.81 us

profile of v5, /device:TPU:0, one launch (start us, length us, event | category | flops | bytes accessed | tf_op | source)
XLA Modules:
  0.0 31.7 jit_solution(16477304304106648454)
XLA Ops:
  1.9 29.0 %shard_map.77 = (f32[1,2,64,1024]{3,2,1,0:T(8,128)S(1)}, f32[4,8,128]{2,1,0:T(8,128)S(1)}) custom-call(bf16[2,1024,1024]{2,1,0:T(8,128)(2,1)} %vis_hbm.1, s32[1]{0:T(128)S(6)} %copy.8.refs_0_, s32[4]{0:T(128)} %refs_1_.1, s32[2,8]{1,0:T(2,128)} %bitcast.1, s32[8]{0:T(128)} %refs_3_.1, s32[1,1]{1,0:T(1,128)S(6)} %copy.9.refs_4_), custom_call_target="tpu_custom_call" | custom-call | tf_op jit(solution)/shard_map/pallas_call | solution.py:444
  30.9 0.8 %shard_map.78 = (f32[1,2,64,1024]{3,2,1,0:T(8,128)}, f32[1]{0:T(128)}) custom-call(f32[1,2,64,1024]{3,2,1,0:T(8,128)S(1)} %get-tuple-element.4.image, f32[4,8,128]{2,1,0:T(8,128)S(1)} %get-tuple-element.5.peaks), custom_call_target="tpu_custom_call" | custom-call | tf_op jit(solution)/shard_map/pallas_call | solution.py:487

commit v6 on v5

--- a/solution.py
+++ b/solution.py
@@ -16,8 +16,8 @@
 FINE = 32
 GROUPS = 4
 ORDER = (
-    "T0", "T1", "R0", "P0", "N0", "T2", "P1", "T3", "P2", "N1", "B0", "B1", "T4", "P3", "N2", "F0", "T5", "P4",
-    "N3", "F1", "T6", "P5", "N4", "B2", "B3", "F2", "T7", "P6", "N5", "R1", "B4", "F3", "P7", "N6", "N7", "B5",
+    "T0", "T1", "R0", "P0", "N0", "T2", "P1", "T3", "N1", "P2", "T4", "B0", "B1", "P3", "N2", "T5", "F0", "P4",
+    "N3", "T6", "F1", "P5", "N4", "T7", "F2", "P6", "N5", "B2", "B3", "P7", "N6", "N7", "F3", "R1", "B4", "B5",
     "B6", "B7", "F4", "E0", "F5", "S0", "F6", "E1", "F7", "S1", "E2", "S2", "H0", "H1", "E3", "S3",
 )
 MESH = pl.DeviceIdType.MESH

time: 31.9 us -> 31.5 us (0.987)
  no operation moved by 1% of the time
where the time goes in v6:
time: 31.5 us; the launch traced here: 31.4 us
  Pallas kernels  29.5 us (94%)
  between operations  1.93 us (6%)
    pallas_call x1, Pallas kernels, local(): pl.pallas_call(functools.partial(kernel, cols, rows, plan), out_shape=(pl...  28.6 us
    pallas_call x1, Pallas kernels, local(): pl.pallas_call(functools.partial(finish_kernel, rows), out_shape=(jax.Sha...  0.81 us

profile of v6, /device:TPU:0, one launch (start us, length us, event | category | flops | bytes accessed | tf_op | source)
XLA Modules:
  0.0 31.4 jit_solution(15433018325844752417)
XLA Ops:
  1.9 28.6 %shard_map.77 = (f32[1,2,64,1024]{3,2,1,0:T(8,128)S(1)}, f32[4,8,128]{2,1,0:T(8,128)S(1)}) custom-call(bf16[2,1024,1024]{2,1,0:T(8,128)(2,1)} %vis_hbm.1, s32[1]{0:T(128)S(6)} %copy.8.refs_0_, s32[4]{0:T(128)} %refs_1_.1, s32[2,8]{1,0:T(2,128)} %bitcast.1, s32[8]{0:T(128)} %refs_3_.1, s32[1,1]{1,0:T(1,128)S(6)} %copy.9.refs_4_), custom_call_target="tpu_custom_call" | custom-call | tf_op jit(solution)/shard_map/pallas_call | solution.py:444
  30.6 0.8 %shard_map.78 = (f32[1,2,64,1024]{3,2,1,0:T(8,128)}, f32[1]{0:T(128)}) custom-call(f32[1,2,64,1024]{3,2,1,0:T(8,128)S(1)} %get-tuple-element.4.image, f32[4,8,128]{2,1,0:T(8,128)S(1)} %get-tuple-element.5.peaks), custom_call_target="tpu_custom_call" | custom-call | tf_op jit(solution)/shard_map/pallas_call | solution.py:487
